TPU v7x, 32 devices: a whole 2x2x4 slice. The times are simulated.
32 devices in a mesh: dp: 8 (over y, x, core), seq: 4 (over z).
Axes of the slice: x: 2, y: 2, z: 4, core: 2. Of those that a mesh axis runs over, the one named last changes fastest.
Arguments:
- tokens: bfloat16 [8, 512, 1024], P('dp', 'seq'), may hold values from -6 to 6
- cotangent: bfloat16 [8, 512, 1024], P('dp', 'seq'), may hold values from -6 to 6
- stamps: int32 [8, 512], P('dp'), may hold values from 0 to 1080832, as said below
- lengths: int32 [8], P('dp'), may hold values from 64 to 512, as said below
- w_qkvu: bfloat16 [1024, 4096], P('dp'), may hold values from -0.1875 to 0.1875
- w_out: bfloat16 [1024, 1024], P('dp'), may hold values from -0.1875 to 0.1875
- gain_in: float32 [1024], replicated, may hold values from 0.25 to 1.75
- gain_out: float32 [1024], replicated, may hold values from 0.25 to 1.75
- bias_table: float32 [8, 16], replicated, may hold values from -4 to 4
Outputs:
- mixed: bfloat16 [8, 512, 1024], P('dp', 'seq')
- input_grad: bfloat16 [8, 512, 1024], P('dp', 'seq')
- out_weight_grad: float32 [1024, 1024], P('dp')
Inputs may be any that keep to these rules, and one draw needn't show every extreme that they name: `lengths`: each stream has 64 valid actions or more; some stream is full. `stamps`: timestamps never fall along a stream, and consecutive ones differ by less than 64.
All inputs are finite; a program needn't handle non-finite values.
Results may differ from a plain program's by a relative error of at most 0.019.
Values may be sent and summed in bfloat16 or wider, within the bound.
A program may use at most 128 MiB of HBM per device.

v0:
```python
import jax
import jax.numpy as jnp
from jax import lax
from jax.sharding import PartitionSpec as P

H = 8
DH = 128
EPS = 1e-05


def layer_norm(values, gain):
    average = jnp.mean(values, axis=-1, keepdims=True)
    centred = values - average
    variance = jnp.mean(centred * centred, axis=-1, keepdims=True)
    return centred * lax.rsqrt(variance + EPS) * gain


def silu_slope(values):
    sigmoid_v = jax.nn.sigmoid(values)
    return sigmoid_v * (1.0 + values * (1.0 - sigmoid_v))


def time_bias(bias_table, stamps_q, stamps_k):
    elapsed = stamps_q[:, None] - stamps_k[None, :]
    bucket = jnp.zeros(elapsed.shape, jnp.int32)
    for degree in range(1, bias_table.shape[1]):
        bucket = bucket + (elapsed >= 2**degree - 1).astype(jnp.int32)
    levels = jnp.arange(bias_table.shape[1], dtype=jnp.int32)
    one_hot = (bucket[:, :, None] == levels[None, None, :]).astype(jnp.float32)
    return jnp.einsum(
        "qkb,hb->hqk",
        one_hot,
        bias_table,
        precision=lax.Precision.HIGHEST,
        preferred_element_type=jnp.float32,
    )


def pair_terms(
    q_heads, d_heads, stamps_q, pos_q, k_heads, v_heads, stamps_k, pos_k, length, bias_table, scale
):
    scores = (
        jnp.einsum("qhd,khd->hqk", q_heads, k_heads, preferred_element_type=jnp.float32) * scale
    )
    scores = scores + time_bias(bias_table, stamps_q, stamps_k)
    allowed = (
        (pos_k[None, :] <= pos_q[:, None]) & (pos_k[None, :] < length) & (pos_q[:, None] < length)
    )
    weight = jnp.where(allowed[None], jax.nn.silu(scores), 0.0).astype(jnp.bfloat16)
    if d_heads is None:
        return (weight, None)
    d_weight = jnp.einsum("qhd,khd->hqk", d_heads, v_heads, preferred_element_type=jnp.float32)
    d_scores = jnp.where(allowed[None], d_weight * silu_slope(scores), 0.0).astype(jnp.bfloat16)
    return (weight, d_scores)


def per_device(tokens, cotangent, stamps, lengths, w_qkvu, w_out, gain_in, gain_out, bias_table):
    rows = tokens[0]
    cot_rows = cotangent[0]
    tok_count = rows.shape[0]
    feature_width = rows.shape[1]
    seq_count = lax.axis_size("seq")
    total_rows = tok_count * seq_count
    first_row = lax.axis_index("seq") * tok_count
    length = lengths[0]
    stamp_all = stamps[0]
    pos_own = first_row + jnp.arange(tok_count, dtype=jnp.int32)
    stamp_own = lax.dynamic_slice_in_dim(stamp_all, first_row, tok_count)
    scale = DH ** (-0.5)
    block_rows = min(512, total_rows)
    block_count = total_rows // block_rows
    w_full, w_out_full = (
        lax.all_gather(w_qkvu, "dp", axis=0, tiled=True),
        lax.all_gather(w_out, "dp", axis=0, tiled=True),
    )
    wide_rows = rows.astype(jnp.float32)
    normed = layer_norm(wide_rows, gain_in).astype(jnp.bfloat16)
    projected = jnp.dot(normed, w_full, preferred_element_type=jnp.float32)
    activated = jax.nn.silu(projected)
    gate_u = activated[:, :feature_width]
    values_own = activated[:, feature_width : 2 * feature_width].astype(jnp.bfloat16)
    queries_own = activated[:, 2 * feature_width : 3 * feature_width].astype(jnp.bfloat16)
    keys_own = activated[:, 3 * feature_width :].astype(jnp.bfloat16)
    keys_all, values_all = (
        lax.all_gather(keys_own, "seq", axis=0, tiled=True),
        lax.all_gather(values_own, "seq", axis=0, tiled=True),
    )
    q_heads = queries_own.reshape(tok_count, H, DH)

    def key_block(start):
        k_heads = lax.dynamic_slice_in_dim(keys_all, start, block_rows).reshape(block_rows, H, DH)
        v_heads = lax.dynamic_slice_in_dim(values_all, start, block_rows).reshape(block_rows, H, DH)
        stamps_k = lax.dynamic_slice_in_dim(stamp_all, start, block_rows)
        pos_k = start + jnp.arange(block_rows, dtype=jnp.int32)
        return (k_heads, v_heads, stamps_k, pos_k)

    def guarded(active, action, state):
        return lax.cond(active, action, lambda same: same, state)

    def reaches(start):
        return (start <= first_row + tok_count - 1) & (start < length) & (first_row < length)

    def forward_step(block_idx, totals):
        start = block_idx * block_rows

        def forward_compute(totals):
            k_heads, v_heads, stamps_k, pos_k = key_block(start)
            weight, unused = pair_terms(
                q_heads,
                None,
                stamp_own,
                pos_own,
                k_heads,
                v_heads,
                stamps_k,
                pos_k,
                length,
                bias_table,
                scale,
            )
            return totals + jnp.einsum(
                "hqk,khd->qhd", weight, v_heads, preferred_element_type=jnp.float32
            )

        return guarded(reaches(start), forward_compute, totals)

    attended = lax.fori_loop(
        0, block_count, forward_step, jnp.zeros((tok_count, H, DH), jnp.float32)
    )
    attended = attended.reshape(tok_count, feature_width)
    normed_att, norm_back = jax.vjp(lambda values: layer_norm(values, gain_out), attended)
    mixed_rows = (normed_att * gate_u).astype(jnp.bfloat16)
    mixed = (
        wide_rows + jnp.dot(mixed_rows, w_out_full, preferred_element_type=jnp.float32)
    ).astype(jnp.bfloat16)
    grad_part = lax.psum_scatter(
        jnp.einsum("tr,tc->rc", mixed_rows, cot_rows, preferred_element_type=jnp.float32).astype(
            jnp.bfloat16
        ),
        "dp",
        scatter_dimension=0,
        tiled=True,
    )
    w_grad = lax.psum(grad_part, "seq").astype(jnp.float32)
    d_mix = jnp.einsum("tc,rc->tr", cot_rows, w_out_full, preferred_element_type=jnp.float32)
    d_gate = d_mix * normed_att
    d_att = norm_back(d_mix * gate_u)[0].astype(jnp.bfloat16)
    d_heads = d_att.reshape(tok_count, H, DH)

    def backward_step():

        def step(block_idx, state_pair):
            start = block_idx * block_rows

            def step_compute(state_pair):
                q_grad, key_terms = state_pair
                k_heads, v_heads, stamps_k, pos_k = key_block(start)
                weight, d_scores = pair_terms(
                    q_heads,
                    d_heads,
                    stamp_own,
                    pos_own,
                    k_heads,
                    v_heads,
                    stamps_k,
                    pos_k,
                    length,
                    bias_table,
                    scale,
                )
                q_grad = (
                    q_grad
                    + jnp.einsum(
                        "hqk,khd->qhd", d_scores, k_heads, preferred_element_type=jnp.float32
                    )
                    * scale
                )
                k_grad = (
                    jnp.einsum(
                        "hqk,qhd->khd", d_scores, q_heads, preferred_element_type=jnp.float32
                    )
                    * scale
                )
                v_grad = jnp.einsum(
                    "hqk,qhd->khd", weight, d_heads, preferred_element_type=jnp.float32
                )
                joined = jnp.concatenate(
                    [
                        k_grad.reshape(block_rows, feature_width),
                        v_grad.reshape(block_rows, feature_width),
                    ],
                    axis=1,
                )
                key_terms = lax.dynamic_update_slice_in_dim(key_terms, joined, start, 0)
                return (q_grad, key_terms)

            return guarded(reaches(start), step_compute, state_pair)

        return step

    q_start = jnp.zeros((tok_count, H, DH), jnp.float32)
    term_start = jnp.zeros((total_rows, 2 * feature_width), jnp.float32)
    q_grad, key_terms = lax.fori_loop(0, block_count, backward_step(), (q_start, term_start))
    key_grads = lax.psum_scatter(
        key_terms.astype(jnp.bfloat16), "seq", scatter_dimension=0, tiled=True
    ).astype(jnp.float32)
    d_act = jnp.concatenate(
        [
            d_gate,
            key_grads[:, feature_width:],
            q_grad.reshape(tok_count, feature_width),
            key_grads[:, :feature_width],
        ],
        axis=1,
    )
    d_proj = (d_act * silu_slope(projected)).astype(jnp.bfloat16)
    d_normed = jnp.einsum("tf,df->td", d_proj, w_full, preferred_element_type=jnp.float32)
    unused_rows, in_back = jax.vjp(lambda values: layer_norm(values, gain_in), wide_rows)
    input_grad = (cot_rows.astype(jnp.float32) + in_back(d_normed)[0]).astype(jnp.bfloat16)
    return (mixed[None], input_grad[None], w_grad)


def solution(mesh):
    return jax.shard_map(
        per_device,
        mesh=mesh,
        in_specs=(
            P("dp", "seq", None),
            P("dp", "seq", None),
            P("dp", None),
            P("dp"),
            P("dp", None),
            P("dp", None),
            P(),
            P(),
            P(),
        ),
        out_specs=(P("dp", "seq", None), P("dp", "seq", None), P("dp", None)),
        check_vma=False,
    )
```

profile of v0, /device:TPU:0, one launch (start us, length us, event | category | flops | bytes accessed | tf_op | source)
XLA Modules:
  0.0 309.4 jit_solution(9463237109078155337)
XLA Ops:
  7.2 0.7 all-gather.5.cloned.1.call-update
  7.9 1.1 convert_reduce_fusion
  9.0 1.2 fusion.49
  10.2 56.7 %all-gather.5.cloned.1.call-done = bf16[1024,4096]{1,0:T(8,128)(2,1)} async-done(((bf16[128,4096]{1,0:T(8,128)(2,1)}), bf16[1024,4096]{1,0:T(8,128)(2,1)}) %all-gather.5.cloned.1.call-update) | async-done | bytes 8388624 | tf_op jit(solution)/shard_map/all_gather | solution.py:73
  66.9 7.0 %fusion.69 = (bf16[128,4096]{1,0:T(8,128)(2,1)S(1)}, f32[128,4096]{1,0:T(8,128)}, f32[128,4096]{1,0:T(8,128)}) fusion(bf16[1024,4096]{1,0:T(8,128)(2,1)} %all-gather.5.cloned.1.call-done, bf16[1,128,1024]{2,1,0:T(8,128)(2,1)} %param.13, f32[1024]{0:T(1024)} %param.19, f32[128]{0:T(128)S(1)} %fusion.63, f32[128]{0:T(128)S(1)} %broadcast_multiply_fusion.1), kind=kOutput, calls=%fused_computation.143 | convolution fusion | flops 1077018624 | bytes 13898752 | tf_op jit(solution)/shard_map/dot_general | solution.py:78
  73.9 0.9 fusion.71
  74.8 0.7 all-gather.9.cloned.1.call-update
  75.6 0.5 all-gather.11.cloned.1.call-update
  76.9 26.0 %all-gather.7.cloned.1.call-done = bf16[512,1024]{1,0:T(8,128)(2,1)} async-done(((bf16[128,1024]{1,0:T(8,128)(2,1)}), bf16[512,1024]{1,0:T(8,128)(2,1)}) %all-gather.7.cloned.1.call-update) | async-done | bytes 1048592 | tf_op jit(solution)/shard_map/all_gather | solution.py:85
  102.9 29.5 %all-gather.9.cloned.1.call-done = bf16[512,1024]{1,0:T(8,128)(2,1)} async-done(((bf16[128,1024]{1,0:T(8,128)(2,1)}), bf16[512,1024]{1,0:T(8,128)(2,1)}) %all-gather.9.cloned.1.call-update) | async-done | bytes 1048592 | tf_op jit(solution)/shard_map/all_gather | solution.py:86
  132.5 8.9 %conditional.2 = (f32[128,8,128]{2,0,1:T(8,128)S(1)}) conditional(s32[]{:T(128)} %convert_element_type.288, f32[128,8,128]{2,0,1:T(8,128)S(1)} %broadcast.484, (s32[128]{0:T(128)S(1)}, s32[]{:T(128)}, bf16[512,1024]{1,0:T(8,128)(2,1)}, bf16[128,8,128]{2,1,0:T(8,128)(2,1)S(1)}, s32[128]{0:T(128)S(1)}, /*index=5*/s32[512]{0:T(512)S(1)}, ...), branch_computations={%region_2.3_spmd, %region_3.0_spmd} | conditional | flops 377619072 | bytes 12457260 | solution.py:98
  132.5 0.5 convert_add_fusion
  133.0 2.7 fusion
  135.7 0.6 broadcast_compare_fusion
  136.3 0.7 iota_compare_fusion.3
  137.1 4.2 %fusion.2 = f32[128,8,128]{2,0,1:T(8,128)S(1)} fusion(f32[128,8,128]{2,0,1:T(8,128)S(1)} %get-tuple-element.155, f32[128,512,8]{1,2,0:T(8,128)} %fusion, pred[128,512]{1,0:T(8,128)(4,1)S(1)} %fusion.16, bf16[128,8,128]{2,1,0:T(8,128)(2,1)S(1)} %get-tuple-element.184, bf16[512,1024]{1,0:T(8,128)(2,1)} %get-tuple-element.163, bf16[512,1024]{1,0:T(8,128)(2,1)S(1)} %copy-done.2), kind=kOutput, calls=%fused_computation.21 | convolution fusion | flops 272760832 | bytes 5570560 | tf_op jit(solution)/shard_map/while/body/eval_jaxpr/cond/branch_1_fun/hqk,khd->qhd/dot_general | solution.py:121
  141.5 0.2 multiply_reduce_fusion.1
  141.7 19.7 %all-gather.11.cloned.1.call-done = bf16[1024,1024]{1,0:T(8,128)(2,1)} async-done(((bf16[128,1024]{1,0:T(8,128)(2,1)}), bf16[1024,1024]{1,0:T(8,128)(2,1)}) %all-gather.11.cloned.1.call-update) | async-done | bytes 2097168 | tf_op jit(solution)/shard_map/all_gather | solution.py:74
  161.4 2.6 multiply_reduce_fusion
  164.0 2.1 fusion.68
  166.2 2.0 convolution_convert_fusion
  168.3 41.2 %reduce-scatter.5.cloned.1.call-done = bf16[128,1024]{1,0:T(8,128)(2,1)} async-done(((bf16[1024,1024]{1,0:T(8,128)(2,1)}), bf16[128,1024]{1,0:T(8,128)(2,1)}) %reduce-scatter.5.cloned.1.call-update) | async-done | bytes 262160 | tf_op jit(solution)/shard_map/reduce_scatter | solution.py:136
  209.7 13.3 %conditional.3 = (bf16[512,2048]{0,1:T(8,128)(2,1)}, f32[128,8,128]{2,0,1:T(8,128)S(1)}) conditional(s32[]{:T(128)} %convert_element_type.288, f32[128,8,128]{2,0,1:T(8,128)S(1)} %broadcast.484, (s32[128]{0:T(128)S(1)}, s32[]{:T(128)}, bf16[128,1024]{1,0:T(8,128)(2,1)S(1)}, bf16[512,1024]{1,0:T(8,128)(2,1)}, bf16[512,1024]{1,0:T(8,128)(2,1)}, ...), branch_computations={%region_8.9_spmd, %region_9.10_spmd} | conditional | flops 790889088 | bytes 37426568 | solution.py:98
  209.9 0.8 copy.23
  210.7 0.5 convert_add_fusion.1
  211.2 1.3 fusion.21
  212.5 1.2 copy.24
  213.7 2.8 bitcast_add_fusion.1
  216.5 0.7 broadcast_compare_fusion.1
  217.2 0.7 iota_compare_fusion.7
  218.0 0.9 fusion.29
  218.8 0.3 copy-done.11
  219.2 1.1 select_convert_fusion.2
  220.3 0.4 convolution_multiply_fusion
  220.8 1.4 pad_maximum_fusion
  222.2 0.2 copy-done.3
  222.4 0.5 fusion.24
  222.9 4.0 %copy.25 = bf16[512,2048]{1,0:T(8,128)(2,1)} copy(bf16[512,2048]{0,1:T(8,128)(2,1)} %get-tuple-element.179) | data formatting | bytes 4194304 | tf_op jit(solution)/shard_map/while/body/eval_jaxpr/cond | solution.py:98
  227.0 1.6 copy-done
  228.5 1.2 fusion.41
  229.8 17.5 %all-reduce.2.cloned.1.call-done = bf16[128,1024]{1,0:T(8,128)(2,1)} async-done(((bf16[128,1024]{1,0:T(8,128)(2,1)}), bf16[128,1024]{1,0:T(8,128)(2,1)}) %all-reduce.2.cloned.1.call-update) | async-done | bytes 262160 | tf_op jit(solution)/shard_map/psum | solution.py:144
  247.3 1.8 convert_element_type.299
  249.1 44.0 %reduce-scatter.3.cloned.1.call-done = bf16[128,2048]{1,0:T(8,128)(2,1)} async-done(((bf16[512,2048]{1,0:T(8,128)(2,1)}), bf16[128,2048]{1,0:T(8,128)(2,1)}) %reduce-scatter.3.cloned.1.call-update) | async-done | bytes 524304 | tf_op jit(solution)/shard_map/reduce_scatter | solution.py:204
  293.1 1.3 fusion.72
  294.4 0.4 copy-done.13
  294.8 6.4 %fusion.52 = (f32[128]{0:T(128)S(1)}, f32[128,1024]{1,0:T(8,128)S(1)}) fusion(bf16[1,128,1024]{2,1,0:T(8,128)(2,1)S(1)} %copy-done.1, f32[128]{0:T(128)S(1)} %broadcast_multiply_fusion.1, f32[1024]{0:T(1024)S(1)} %copy-done.12, bf16[1024,4096]{1,0:T(8,128)(2,1)} %all-gather.5.cloned.1.call-done, f32[128,1024]{1,0:T(8,128)S(1)} %get-tuple-element.210, ...), kind=kOutput, calls=%fused_computation.107 | convolution fusion | flops 1080688512 | bytes 13374464 | tf_op jit(solution)/shard_map/tf,df->td/dot_general | solution.py:217
  301.3 0.3 fusion.67
  301.6 1.0 fusion.54
  (51 shorter events, 1.0 us)
Async XLA Ops:
  7.2 59.7 %all-gather.5.cloned.1.call-start = ((), (), s32[]{:S(2)}) async-start(), calls=%async_computation.2 | async-start | bytes 9437184 | tf_op jit(solution)/shard_map/all_gather | solution.py:73
  7.9 95.0 %all-gather.7.cloned.1.call-start = ((), (), s32[]{:S(2)}) async-start(), calls=%async_computation.3 | async-start | bytes 1310720 | tf_op jit(solution)/shard_map/all_gather | solution.py:85
  73.9 2.9 copy-start.10
  73.9 58.6 %copy-start.9 = (f32[8,16]{1,0:T(8,128)S(1)}, f32[8,16]{1,0:T(8,128)}, u32[]{:S(2)}) copy-start(f32[8,16]{1,0:T(8,128)} %param.21) | copy-start | bytes 1540
  74.8 57.7 %all-gather.9.cloned.1.call-start = ((), (), s32[]{:S(2)}) async-start(), calls=%async_computation.4 | async-start | bytes 1310720 | tf_op jit(solution)/shard_map/all_gather | solution.py:86
  75.5 85.9 %all-gather.11.cloned.1.call-start = ((), (), s32[]{:S(2)}) async-start(), calls=%async_computation.5 | async-start | bytes 2359296 | tf_op jit(solution)/shard_map/all_gather | solution.py:74
  76.1 133.4 %reduce-scatter.5.cloned.1.call-start = ((), (), s32[]{:S(2)}) async-start(), calls=%async_computation.7 | async-start | bytes 2359296 | tf_op jit(solution)/shard_map/reduce_scatter | solution.py:136
  132.5 28.9 %copy-start.4 = (bf16[1,128,1024]{2,1,0:T(8,128)(2,1)S(1)}, bf16[1,128,1024]{2,1,0:T(8,128)(2,1)}, u32[]{:S(2)}) copy-start(bf16[1,128,1024]{2,1,0:T(8,128)(2,1)} %param.14) | copy-start | bytes 786436
  132.5 28.9 %copy-start.8 = (f32[1024]{0:T(1024)S(1)}, f32[1024]{0:T(1024)}, u32[]{:S(2)}) copy-start(f32[1024]{0:T(1024)} %param.20) | copy-start | bytes 12292
  132.5 4.6 %copy-start.2 = (bf16[512,1024]{1,0:T(8,128)(2,1)S(1)}, bf16[512,1024]{1,0:T(8,128)(2,1)}, u32[]{:S(2)}) copy-start(bf16[512,1024]{1,0:T(8,128)(2,1)} %get-tuple-element.159) | copy-start | bytes 3145732 | tf_op jit(solution)/shard_map/while/body/eval_jaxpr/cond
  168.2 79.1 %all-reduce.2.cloned.1.call-start = ((), (), s32[]{:S(2)}) async-start(), calls=%async_computation.8 | async-start | bytes 524288 | tf_op jit(solution)/shard_map/psum | solution.py:144
  209.5 83.6 %reduce-scatter.3.cloned.1.call-start = ((), (), s32[]{:S(2)}) async-start(), calls=%async_computation.6 | async-start | bytes 2621440 | tf_op jit(solution)/shard_map/reduce_scatter | solution.py:204
  209.9 1.3 copy-start.5
  213.7 4.3 %copy-start.7 = (bf16[128,1024]{0,1:T(8,128)(2,1)S(1)}, bf16[128,1024]{0,1:T(8,128)(2,1)}, u32[]{:S(2)}) copy-start(bf16[128,1024]{0,1:T(8,128)(2,1)} %copy.23) | copy-start | bytes 786436 | tf_op jit(solution)/shard_map/while/body/eval_jaxpr/cond
  218.0 1.2 copy-start.11
  220.8 1.6 copy-start.3
  222.9 4.1 %copy-start.1 = (bf16[1,128,1024]{2,1,0:T(8,128)(2,1)S(1)}, bf16[1,128,1024]{2,1,0:T(8,128)(2,1)}, u32[]{:S(2)}) copy-start(bf16[1,128,1024]{2,1,0:T(8,128)(2,1)} %param.13) | copy-start | bytes 786436
  226.9 1.6 copy-start
  229.7 64.7 %copy-start.6 = (f32[128,1024]{1,0:T(8,128)S(1)}, f32[128,1024]{1,0:T(8,128)}, u32[]{:S(2)}) copy-start(f32[128,1024]{1,0:T(8,128)} %get-tuple-element.205) | copy-start | bytes 1572868
  229.7 64.7 %copy-start.12 = (f32[1024]{0:T(1024)S(1)}, f32[1024]{0:T(1024)}, u32[]{:S(2)}) copy-start(f32[1024]{0:T(1024)} %param.19) | copy-start | bytes 12292
  293.1 1.7 copy-start.13
Sparse Core Ops, SparseCore 0:
  9.9 56.9 all-gather.4
  74.9 27.9 all-gather.6
  105.1 27.3 all-gather.8
  134.2 27.1 all-gather.10
  168.3 41.0 reduce-scatter.4
  211.7 35.5 all-reduce.1
  249.6 43.4 reduce-scatter.2
where the time goes:
time: 310 us; the launch traced here: 309 us
  waiting for transfers between devices  237 us (76%)
  matrix products  33.2 us (11%)
  between operations  14.9 us (5%)
  other arithmetic  13.1 us (4%)
  local copies, waits for them, and re-layouts  10.9 us (4%)
    all_gather x1, waiting for transfers between devices, per_device(): lax.all_gather(w_qkvu, 'dp', axis=0, tiled=True)  56.7 us
    reduce_scatter x1, waiting for transfers between devices, per_device(): lax.psum_scatter(key_terms.astype(jnp.bfloat16), 'seq', scatter_dimension...  44 us
    reduce_scatter x1, waiting for transfers between devices, per_device(): lax.psum_scatter(jnp.einsum('tr,tc->rc', mixed_rows, cot_rows, preferred_...  41.2 us
    all_gather x1, waiting for transfers between devices, per_device(): lax.all_gather(values_own, 'seq', axis=0, tiled=True)  29.5 us
    all_gather x1, waiting for transfers between devices, per_device(): lax.all_gather(keys_own, 'seq', axis=0, tiled=True)  26 us
    all_gather x1, waiting for transfers between devices, per_device(): lax.all_gather(w_out, 'dp', axis=0, tiled=True)  19.7 us
    psum x1, waiting for transfers between devices, per_device(): w_grad = lax.psum(grad_part, 'seq').astype(jnp.float32)  17.5 us
    dot_general x1, matrix products, per_device(): projected = jnp.dot(normed, w_full, preferred_element_type=jnp.float32)  7 us
  transfers between devices with their start and end apart: 7, of which 7 were waited for; matrix products, arithmetic and copies ran while one was open for 10% of the time, Pallas kernels for 0%

commit v1 on v0

--- a/solution.py
+++ b/solution.py
@@ -141,7 +141,7 @@
         scatter_dimension=0,
         tiled=True,
     )
-    w_grad = lax.psum(grad_part, "seq").astype(jnp.float32)
+    w_grad = jnp.sum(lax.all_gather(grad_part, "seq"), axis=0).astype(jnp.float32)
     d_mix = jnp.einsum("tc,rc->tr", cot_rows, w_out_full, preferred_element_type=jnp.float32)
     d_gate = d_mix * normed_att
     d_att = norm_back(d_mix * gate_u)[0].astype(jnp.bfloat16)

time: 310 us -> 294 us (0.948)
  waiting for transfers between devices: 237 us -> 220 us
    reduce_scatter x1, waiting for transfers between devices: 41.2 us -> 20.8 us  [per_device(): lax.psum_scatter(jnp.einsum('tr,tc->rc', mixed_rows, cot_rows, preferred_...]
    all_gather x0 -> x1, waiting for transfers between devices: none -> 19.4 us  [per_device(): lax.all_gather(grad_part, 'seq')]
    psum x1 -> x0, waiting for transfers between devices: 17.5 us -> none  [per_device(): w_grad = lax.psum(grad_part, 'seq').astype(jnp.float32)]
  transfers between devices with their start and end apart: 7 -> 7, of which waited for: 7 -> 7; matrix products, arithmetic and copies ran while one was open for 10% -> 13% of each run, Pallas kernels for 0% -> 0%
where the time goes in v1:
time: 294 us; the launch traced here: 293 us
  waiting for transfers between devices  220 us (75%)
  matrix products  33.1 us (11%)
  between operations  15 us (5%)
  other arithmetic  13.6 us (5%)
  local copies, waits for them, and re-layouts  10.9 us (4%)
    all_gather x1, waiting for transfers between devices, per_device(): lax.all_gather(w_qkvu, 'dp', axis=0, tiled=True)  56.7 us
    reduce_scatter x1, waiting for transfers between devices, per_device(): lax.psum_scatter(key_terms.astype(jnp.bfloat16), 'seq', scatter_dimension...  45.8 us
    all_gather x1, waiting for transfers between devices, per_device(): lax.all_gather(values_own, 'seq', axis=0, tiled=True)  29.5 us
    all_gather x1, waiting for transfers between devices, per_device(): lax.all_gather(keys_own, 'seq', axis=0, tiled=True)  26 us
    reduce_scatter x1, waiting for transfers between devices, per_device(): lax.psum_scatter(jnp.einsum('tr,tc->rc', mixed_rows, cot_rows, preferred_...  20.8 us
    all_gather x1, waiting for transfers between devices, per_device(): lax.all_gather(w_out, 'dp', axis=0, tiled=True)  19.7 us
    all_gather x1, waiting for transfers between devices, per_device(): lax.all_gather(grad_part, 'seq')  19.4 us
    dot_general x1, matrix products, per_device(): projected = jnp.dot(normed, w_full, preferred_element_type=jnp.float32)  6.91 us
  transfers between devices with their start and end apart: 7, of which 7 were waited for; matrix products, arithmetic and copies ran while one was open for 13% of the time, Pallas kernels for 0%

profile of v1, /device:TPU:0, one launch (start us, length us, event | category | flops | bytes accessed | tf_op | source)
XLA Modules:
  0.0 293.1 jit_solution(1874775157418746528)
XLA Ops:
  7.2 0.7 all-gather.7.cloned.1.call-update
  7.9 1.1 convert_reduce_fusion
  9.0 1.2 fusion.49
  10.2 56.7 %all-gather.7.cloned.1.call-done = bf16[1024,4096]{1,0:T(8,128)(2,1)} async-done(((bf16[128,4096]{1,0:T(8,128)(2,1)}), bf16[1024,4096]{1,0:T(8,128)(2,1)}) %all-gather.7.cloned.1.call-update) | async-done | bytes 8388624 | tf_op jit(solution)/shard_map/all_gather | solution.py:73
  66.9 6.9 %fusion.69 = (bf16[128,4096]{1,0:T(8,128)(2,1)S(1)}, f32[128,4096]{1,0:T(8,128)}, f32[128,4096]{1,0:T(8,128)}) fusion(bf16[1024,4096]{1,0:T(8,128)(2,1)} %all-gather.7.cloned.1.call-done, bf16[1,128,1024]{2,1,0:T(8,128)(2,1)} %param.13, f32[1024]{0:T(1024)} %param.19, f32[128]{0:T(128)S(1)} %fusion.63, f32[128]{0:T(128)S(1)} %broadcast_multiply_fusion.1), kind=kOutput, calls=%fused_computation.143 | convolution fusion | flops 1077018624 | bytes 13898752 | tf_op jit(solution)/shard_map/dot_general | solution.py:78
  73.8 0.9 fusion.71
  74.7 0.7 all-gather.11.cloned.1.call-update
  75.5 0.5 all-gather.13.cloned.1.call-update
  76.8 26.0 %all-gather.9.cloned.1.call-done = bf16[512,1024]{1,0:T(8,128)(2,1)} async-done(((bf16[128,1024]{1,0:T(8,128)(2,1)}), bf16[512,1024]{1,0:T(8,128)(2,1)}) %all-gather.9.cloned.1.call-update) | async-done | bytes 1048592 | tf_op jit(solution)/shard_map/all_gather | solution.py:85
  102.8 29.5 %all-gather.11.cloned.1.call-done = bf16[512,1024]{1,0:T(8,128)(2,1)} async-done(((bf16[128,1024]{1,0:T(8,128)(2,1)}), bf16[512,1024]{1,0:T(8,128)(2,1)}) %all-gather.11.cloned.1.call-update) | async-done | bytes 1048592 | tf_op jit(solution)/shard_map/all_gather | solution.py:86
  132.4 8.9 %conditional.2 = (f32[128,8,128]{2,0,1:T(8,128)S(1)}) conditional(s32[]{:T(128)} %convert_element_type.290, f32[128,8,128]{2,0,1:T(8,128)S(1)} %broadcast.484, (s32[128]{0:T(128)S(1)}, s32[]{:T(128)}, bf16[512,1024]{1,0:T(8,128)(2,1)}, bf16[128,8,128]{2,1,0:T(8,128)(2,1)S(1)}, s32[128]{0:T(128)S(1)}, /*index=5*/s32[512]{0:T(512)S(1)}, ...), branch_computations={%region_2.3_spmd, %region_3.0_spmd} | conditional | flops 377619072 | bytes 12457260 | solution.py:98
  132.5 0.5 convert_add_fusion
  132.9 2.7 fusion
  135.6 0.6 broadcast_compare_fusion
  136.3 0.7 iota_compare_fusion.3
  137.1 4.2 %fusion.2 = f32[128,8,128]{2,0,1:T(8,128)S(1)} fusion(f32[128,8,128]{2,0,1:T(8,128)S(1)} %get-tuple-element.155, f32[128,512,8]{1,2,0:T(8,128)} %fusion, pred[128,512]{1,0:T(8,128)(4,1)S(1)} %fusion.16, bf16[128,8,128]{2,1,0:T(8,128)(2,1)S(1)} %get-tuple-element.184, bf16[512,1024]{1,0:T(8,128)(2,1)} %get-tuple-element.163, bf16[512,1024]{1,0:T(8,128)(2,1)S(1)} %copy-done.2), kind=kOutput, calls=%fused_computation.21 | convolution fusion | flops 272760832 | bytes 5570560 | tf_op jit(solution)/shard_map/while/body/eval_jaxpr/cond/branch_1_fun/hqk,khd->qhd/dot_general | solution.py:121
  141.6 19.7 %all-gather.13.cloned.1.call-done = bf16[1024,1024]{1,0:T(8,128)(2,1)} async-done(((bf16[128,1024]{1,0:T(8,128)(2,1)}), bf16[1024,1024]{1,0:T(8,128)(2,1)}) %all-gather.13.cloned.1.call-update) | async-done | bytes 2097168 | tf_op jit(solution)/shard_map/all_gather | solution.py:74
  161.3 2.6 multiply_reduce_fusion
  163.9 2.1 fusion.68
  166.1 2.0 convolution_convert_fusion
  168.3 13.5 %conditional.3 = (bf16[512,2048]{0,1:T(8,128)(2,1)}, f32[128,8,128]{2,0,1:T(8,128)S(1)}) conditional(s32[]{:T(128)} %convert_element_type.290, f32[128,8,128]{2,0,1:T(8,128)S(1)} %broadcast.484, (s32[128]{0:T(128)S(1)}, s32[]{:T(128)}, bf16[128,1024]{1,0:T(8,128)(2,1)S(1)}, bf16[512,1024]{1,0:T(8,128)(2,1)}, bf16[512,1024]{1,0:T(8,128)(2,1)}, ...), branch_computations={%region_8.9_spmd, %region_9.10_spmd} | conditional | flops 790889088 | bytes 37426568 | solution.py:98
  168.5 0.8 copy.23
  169.3 0.5 convert_add_fusion.1
  169.8 1.3 fusion.21
  171.1 1.2 copy.24
  172.3 2.8 bitcast_add_fusion.1
  175.1 0.7 broadcast_compare_fusion.1
  175.8 0.7 iota_compare_fusion.7
  176.6 0.9 fusion.29
  177.5 0.4 copy-done.11
  177.9 1.1 select_convert_fusion.2
  179.0 0.4 convolution_multiply_fusion
  179.5 1.5 pad_maximum_fusion
  180.9 0.3 copy-done.3
  181.2 0.5 fusion.24
  181.8 4.0 %copy.25 = bf16[512,2048]{1,0:T(8,128)(2,1)} copy(bf16[512,2048]{0,1:T(8,128)(2,1)} %get-tuple-element.179) | data formatting | bytes 4194304 | tf_op jit(solution)/shard_map/while/body/eval_jaxpr/cond | solution.py:98
  185.9 1.5 copy-done
  187.4 1.2 fusion.41
  188.6 20.8 %reduce-scatter.5.cloned.1.call-done = bf16[128,1024]{1,0:T(8,128)(2,1)} async-done(((bf16[1024,1024]{1,0:T(8,128)(2,1)}), bf16[128,1024]{1,0:T(8,128)(2,1)}) %reduce-scatter.5.cloned.1.call-update) | async-done | bytes 262160 | tf_op jit(solution)/shard_map/reduce_scatter | solution.py:136
  209.4 45.8 %reduce-scatter.3.cloned.1.call-done = bf16[128,2048]{1,0:T(8,128)(2,1)} async-done(((bf16[512,2048]{1,0:T(8,128)(2,1)}), bf16[128,2048]{1,0:T(8,128)(2,1)}) %reduce-scatter.3.cloned.1.call-update) | async-done | bytes 524304 | tf_op jit(solution)/shard_map/reduce_scatter | solution.py:204
  255.2 1.3 fusion.72
  256.5 0.4 copy-done.13
  256.9 6.4 %fusion.52 = (f32[128]{0:T(128)S(1)}, f32[128,1024]{1,0:T(8,128)S(1)}) fusion(bf16[1,128,1024]{2,1,0:T(8,128)(2,1)S(1)} %copy-done.1, f32[128]{0:T(128)S(1)} %broadcast_multiply_fusion.1, f32[1024]{0:T(1024)S(1)} %copy-done.12, bf16[1024,4096]{1,0:T(8,128)(2,1)} %all-gather.7.cloned.1.call-done, f32[128,1024]{1,0:T(8,128)S(1)} %get-tuple-element.210, ...), kind=kOutput, calls=%fused_computation.107 | convolution fusion | flops 1080688512 | bytes 13374464 | tf_op jit(solution)/shard_map/tf,df->td/dot_general | solution.py:217
  263.3 0.3 fusion.67
  263.6 1.0 fusion.54
  264.6 19.4 %all-gather.15.cloned.1.call-done = bf16[512,1024]{1,0:T(8,128)(2,1)} async-done(((bf16[128,1024]{1,0:T(8,128)(2,1)}), bf16[512,1024]{1,0:T(8,128)(2,1)}) %all-gather.15.cloned.1.call-update) | async-done | bytes 1048592 | tf_op jit(solution)/shard_map/all_gather | solution.py:144
  284.0 1.4 reduce_sum.98
  285.4 0.8 convert_element_type.301
  (52 shorter events, 1.3 us)
Async XLA Ops:
  7.2 59.7 %all-gather.7.cloned.1.call-start = ((), (), s32[]{:S(2)}) async-start(), calls=%async_computation.2 | async-start | bytes 9437184 | tf_op jit(solution)/shard_map/all_gather | solution.py:73
  7.9 94.9 %all-gather.9.cloned.1.call-start = ((), (), s32[]{:S(2)}) async-start(), calls=%async_computation.3 | async-start | bytes 1310720 | tf_op jit(solution)/shard_map/all_gather | solution.py:85
  73.8 2.9 copy-start.10
  73.8 58.6 %copy-start.9 = (f32[8,16]{1,0:T(8,128)S(1)}, f32[8,16]{1,0:T(8,128)}, u32[]{:S(2)}) copy-start(f32[8,16]{1,0:T(8,128)} %param.21) | copy-start | bytes 1540
  74.7 57.7 %all-gather.11.cloned.1.call-start = ((), (), s32[]{:S(2)}) async-start(), calls=%async_computation.4 | async-start | bytes 1310720 | tf_op jit(solution)/shard_map/all_gather | solution.py:86
  75.4 85.9 %all-gather.13.cloned.1.call-start = ((), (), s32[]{:S(2)}) async-start(), calls=%async_computation.5 | async-start | bytes 2359296 | tf_op jit(solution)/shard_map/all_gather | solution.py:74
  76.0 133.4 %reduce-scatter.5.cloned.1.call-start = ((), (), s32[]{:S(2)}) async-start(), calls=%async_computation.7 | async-start | bytes 2359296 | tf_op jit(solution)/shard_map/reduce_scatter | solution.py:136
  132.4 28.9 %copy-start.4 = (bf16[1,128,1024]{2,1,0:T(8,128)(2,1)S(1)}, bf16[1,128,1024]{2,1,0:T(8,128)(2,1)}, u32[]{:S(2)}) copy-start(bf16[1,128,1024]{2,1,0:T(8,128)(2,1)} %param.14) | copy-start | bytes 786436
  132.4 28.9 %copy-start.8 = (f32[1024]{0:T(1024)S(1)}, f32[1024]{0:T(1024)}, u32[]{:S(2)}) copy-start(f32[1024]{0:T(1024)} %param.20) | copy-start | bytes 12292
  132.4 4.6 %copy-start.2 = (bf16[512,1024]{1,0:T(8,128)(2,1)S(1)}, bf16[512,1024]{1,0:T(8,128)(2,1)}, u32[]{:S(2)}) copy-start(bf16[512,1024]{1,0:T(8,128)(2,1)} %get-tuple-element.159) | copy-start | bytes 3145732 | tf_op jit(solution)/shard_map/while/body/eval_jaxpr/cond
  168.1 87.1 %reduce-scatter.3.cloned.1.call-start = ((), (), s32[]{:S(2)}) async-start(), calls=%async_computation.6 | async-start | bytes 2621440 | tf_op jit(solution)/shard_map/reduce_scatter | solution.py:204
  168.5 1.3 copy-start.5
  172.3 4.3 %copy-start.7 = (bf16[128,1024]{0,1:T(8,128)(2,1)S(1)}, bf16[128,1024]{0,1:T(8,128)(2,1)}, u32[]{:S(2)}) copy-start(bf16[128,1024]{0,1:T(8,128)(2,1)} %copy.23) | copy-start | bytes 786436 | tf_op jit(solution)/shard_map/while/body/eval_jaxpr/cond
  176.6 1.3 copy-start.11
  179.4 1.8 copy-start.3
  181.7 4.1 %copy-start.1 = (bf16[1,128,1024]{2,1,0:T(8,128)(2,1)S(1)}, bf16[1,128,1024]{2,1,0:T(8,128)(2,1)}, u32[]{:S(2)}) copy-start(bf16[1,128,1024]{2,1,0:T(8,128)(2,1)} %param.13) | copy-start | bytes 786436
  185.8 1.6 copy-start
  185.8 98.2 %all-gather.15.cloned.1.call-start = ((), (), s32[]{:S(2)}) async-start(), calls=%async_computation.8 | async-start | bytes 1310720 | tf_op jit(solution)/shard_map/all_gather | solution.py:144
  188.5 68.0 %copy-start.6 = (f32[128,1024]{1,0:T(8,128)S(1)}, f32[128,1024]{1,0:T(8,128)}, u32[]{:S(2)}) copy-start(f32[128,1024]{1,0:T(8,128)} %get-tuple-element.205) | copy-start | bytes 1572868
  188.5 68.0 %copy-start.12 = (f32[1024]{0:T(1024)S(1)}, f32[1024]{0:T(1024)}, u32[]{:S(2)}) copy-start(f32[1024]{0:T(1024)} %param.19) | copy-start | bytes 12292
  255.2 1.7 copy-start.13
Sparse Core Ops, SparseCore 0:
  9.9 56.9 all-gather.6
  74.8 27.9 all-gather.8
  105.0 27.3 all-gather.10
  134.1 27.1 all-gather.12
  168.2 41.0 reduce-scatter.4
  211.5 43.6 reduce-scatter.2
  256.7 27.1 all-gather.14
